TPU v7x, 32 devices: a whole 2x2x4 slice. The times are simulated.
32 devices in a mesh: dp: 4 (over y, x), expert: 8 (over z, core).
Axes of the slice: x: 2, y: 2, z: 4, core: 2. Of those that a mesh axis runs over, the one named last changes fastest.
Arguments:
- hidden: bfloat16 [8, 4608, 1408], P('expert', 'dp')
- upstream: bfloat16 [8, 4608, 2048], P('expert', 'dp')
- token_counts: int32 [8, 4], P('expert', 'dp'), may hold values from 1 to 1152, as said below
- master: float32 [8, 1408, 2048], P('expert', 'dp'), may hold values from -0.15625 to 0.15625
- first_moment: float32 [8, 1408, 2048], P('expert', 'dp'), may hold values from -6 to 6
- second_moment: float32 [8, 1408, 2048], P('expert', 'dp'), may hold values from 0.25 to 4
- router_input: bfloat16 [4096, 2048], P(('dp', 'expert')), may hold values from -6 to 6
- router_cot: bfloat16 [64, 4096], P(None, ('dp', 'expert'))
- router_master: float32 [64, 2048], replicated, may hold values from -0.125 to 0.125
- router_first: float32 [64, 2048], replicated, may hold values from -6 to 6
- router_second: float32 [64, 2048], replicated, may hold values from 0.25 to 4
- partner: int32 [8], replicated, may hold values from 0 to 7, as said below
Outputs:
- new_weight: bfloat16 [8, 1408, 2048], P('expert')
- new_master: float32 [8, 1408, 2048], P('expert', 'dp')
- new_first: float32 [8, 1408, 2048], P('expert', 'dp')
- new_second: float32 [8, 1408, 2048], P('expert', 'dp')
- router_master_new: float32 [64, 2048], replicated
- router_first_new: float32 [64, 2048], replicated
- router_second_new: float32 [64, 2048], replicated
Inputs may be any that keep to these rules, and one draw needn't show every extreme that they name: partner[partner[p]] = p for every position p; a position with partner[p] = p keeps its expert. The first token_counts[e, d] of replica d's 1152 slots for position e are live, the rest are padding.
All inputs are finite; a program needn't handle non-finite values.
Results may differ from a plain program's by a relative error of at most 0.001.
Values may be sent and summed in bfloat16 or wider, within the bound.
A program may use at most 128 MiB of HBM per device.

v0:
```python
import math
import jax
import jax.numpy as jnp
from jax import lax
from jax.sharding import PartitionSpec as P

beta_first = 0.9
beta_second = 0.95
learn_rate = 0.001
decay_weight = 0.1
adam_eps = 1e-08
norm_eps = 1e-06
correct_first = 1.0 - 0.9**10
correct_second = 1.0 - 0.95**10


def adam_update(gradient, moment_one, moment_two, weights):
    first_new = beta_first * moment_one + (1.0 - beta_first) * gradient
    second_new = beta_second * moment_two + (1.0 - beta_second) * gradient * gradient
    ratio = first_new / correct_first / (jnp.sqrt(second_new / correct_second) + adam_eps)
    weights_new = weights - learn_rate * (ratio + decay_weight * weights)
    return (weights_new, first_new, second_new)


def split_pieces(matrix, groups):
    return matrix.reshape(matrix.shape[0], groups, matrix.shape[1] // groups)


def relocate_state(states, partner):
    groups = lax.axis_size("expert")
    pieces = tuple((split_pieces(member, groups) for member in states))

    def reorder(received):
        arranged = tuple((jnp.take(member, partner, axis=1) for member in received))
        return lax.all_to_all(arranged, "expert", split_axis=1, concat_axis=1, tiled=True)

    result = reorder(
        (
            lax.all_to_all(pieces[0], "expert", split_axis=1, concat_axis=1, tiled=True),
            lax.all_to_all(pieces[1], "expert", split_axis=1, concat_axis=1, tiled=True),
            lax.all_to_all(pieces[2], "expert", split_axis=1, concat_axis=1, tiled=True),
        )
    )
    return tuple((member.reshape(member.shape[0], -1) for member in result))


def regather(weight_shard):
    return lax.all_gather(weight_shard, "dp", axis=0, tiled=True)


def on_device(
    hidden,
    upstream,
    token_counts,
    master,
    first_moment,
    second_moment,
    router_input,
    router_cot,
    router_master,
    router_first,
    router_second,
    partner,
):
    hidden_units = hidden.shape[2]
    features = upstream.shape[2]
    row_count = hidden.shape[1]
    live_rows = jnp.arange(row_count, dtype=jnp.int32) < token_counts[0, 0]
    activations = hidden[0]
    grads_out = upstream[0]
    masked_out = jnp.where(live_rows[:, None], grads_out, jnp.zeros_like(grads_out))
    router_partial = jnp.dot(router_cot, router_input, preferred_element_type=jnp.float32)
    gradient = lax.psum_scatter(
        lax.dot_general(
            activations, masked_out, (((0,), (0,)), ((), ())), preferred_element_type=jnp.float32
        ),
        "dp",
        scatter_dimension=0,
        tiled=True,
    )
    router_grad, expert_square = lax.psum(
        (router_partial, jnp.sum(gradient * gradient)), ("dp", "expert")
    )
    total_square = expert_square + jnp.sum(router_grad * router_grad)
    clip_limit = 2.0 * math.sqrt(
        float(lax.axis_size("expert") * hidden_units * features + router_cot.shape[0] * features)
    )
    factor = jnp.minimum(1.0, clip_limit / (jnp.sqrt(total_square) + norm_eps))
    master_new, first_new, second_new = adam_update(
        factor * gradient, first_moment[0], second_moment[0], master[0]
    )
    router_outs = adam_update(factor * router_grad, router_first, router_second, router_master)
    moved = relocate_state((master_new, first_new, second_new), partner)
    moved_weight = regather(moved[0].astype(jnp.bfloat16))
    return (
        moved_weight[None],
        moved[0][None],
        moved[1][None],
        moved[2][None],
        router_outs[0],
        router_outs[1],
        router_outs[2],
    )


def solution(mesh):
    in_specs = (
        P("expert", "dp", None),
        P("expert", "dp", None),
        P("expert", "dp"),
        P("expert", "dp", None),
        P("expert", "dp", None),
        P("expert", "dp", None),
        P(("dp", "expert"), None),
        P(None, ("dp", "expert")),
        P(),
        P(),
        P(),
        P(),
    )
    out_specs = (
        P("expert", None, None),
        P("expert", "dp", None),
        P("expert", "dp", None),
        P("expert", "dp", None),
        P(),
        P(),
        P(),
    )
    return jax.shard_map(
        on_device, mesh=mesh, in_specs=in_specs, out_specs=out_specs, check_vma=False
    )
```

profile of v0, /device:TPU:0, one launch (start us, length us, event | category | flops | bytes accessed | tf_op | source)
XLA Modules:
  0.0 716.0 jit_solution(1665810783923439618)
XLA Ops:
  9.9 12.9 %convolution_bitcast_fusion = f32[1408,2048]{0,1:T(8,128)} fusion(bf16[1,1152,2048]{2,1,0:T(8,128)(2,1)} %param.15, pred[1152]{0:T(1024)(128)(4,1)S(1)} %iota_compare_fusion, bf16[1,1152,1408]{2,1,0:T(8,128)(2,1)S(1)} %copy-done), kind=kOutput, calls=%fused_computation.3 | convolution fusion | flops 6646136832 | bytes 19498112 | tf_op jit(solution)/shard_map/dot_general | solution.py:74
  22.8 12.0 %copy.42 = f32[1408,2048]{1,0:T(8,128)} copy(f32[1408,2048]{0,1:T(8,128)} %convolution_bitcast_fusion) | data formatting | bytes 23068672
  40.1 3.6 copy.33
  46.2 105.0 %reduce-scatter.4.cloned.1.call-done = f32[352,2048]{1,0:T(8,128)} async-done(((f32[1408,2048]{1,0:T(8,128)}), f32[352,2048]{1,0:T(8,128)}) %reduce-scatter.4.cloned.1.call-update) | async-done | bytes 2883600
  154.9 58.7 %all-reduce.2.cloned.1.call-done = f32[64,2048]{1,0:T(8,128)} async-done(((f32[64,2048]{1,0:T(8,128)}), f32[64,2048]{1,0:T(8,128)}) %all-reduce.2.cloned.1.call-update) | async-done | bytes 524304 | tf_op jit(solution)/shard_map/psum | solution.py:81
  215.4 39.5 %psum.14 = f32[]{:T(128)} all-reduce(f32[]{:T(128)} %multiply_reduce_fusion), channel_id=1, replica_groups=mesh['dp'=4,'expert'=8] {'dp','expert'}, use_global_device_ids=true, to_apply=%region_2.3 | all-reduce | flops 1 | bytes 8 | tf_op jit(solution)/shard_map/psum | solution.py:81
  256.2 6.9 bitcast_subtract_fusion
  266.6 4.7 all-to-all-start
  273.5 63.6 %all-to-all-done = f32[352,8,256]{2,0,1:T(8,128)} async-done(((f32[352,8,256]{2,0,1:T(8,128)}), f32[352,8,256]{2,0,1:T(8,128)}, u32[]{:S(2)}, u32[]{:S(2)}) %all-to-all-start) | async-done | bytes 2883616 | tf_op jit(solution)/shard_map/all_to_all | solution.py:39
  337.1 4.4 all-to-all-start.2
  343.9 63.6 %all-to-all-done.2 = f32[352,8,256]{2,0,1:T(8,128)} async-done(((f32[352,8,256]{2,0,1:T(8,128)}), f32[352,8,256]{2,0,1:T(8,128)}, u32[]{:S(2)}, u32[]{:S(2)}) %all-to-all-start.2) | async-done | bytes 2883616 | tf_op jit(solution)/shard_map/all_to_all | solution.py:40
  407.5 4.6 all-to-all-start.4
  414.7 4.1 gather_fusion.1
  418.8 59.0 %all-to-all-done.4 = f32[352,8,256]{2,0,1:T(8,128)} async-done(((f32[352,8,256]{2,0,1:T(8,128)}), f32[352,8,256]{2,0,1:T(8,128)}, u32[]{:S(2)}, u32[]{:S(2)}) %all-to-all-start.4) | async-done | bytes 2883616 | tf_op jit(solution)/shard_map/all_to_all | solution.py:41
  477.8 4.1 gather_fusion.2
  481.9 6.0 select_bitcast_fusion
  487.9 68.3 %all_to_all.30 = f32[352,8,256]{2,0,1:T(8,128)S(1)} all-to-all(f32[352,8,256]{2,0,1:T(8,128)S(1)} %get-tuple-element.16), channel_id=1, replica_groups=mesh['dp'=4,'expert'=8] {'expert'}, dimensions={1} | all-to-all | bytes 5767168 | tf_op jit(solution)/shard_map/all_to_all | solution.py:35
  556.3 4.4 all-to-all-start.3
  562.2 64.4 %all-to-all-done.3 = f32[352,8,256]{2,0,1:T(8,128)} async-done(((f32[352,8,256]{2,0,1:T(8,128)}), f32[352,8,256]{2,0,1:T(8,128)}, u32[]{:S(2)}, u32[]{:S(2)}) %all-to-all-start.3) | async-done | bytes 2883616 | tf_op jit(solution)/shard_map/all_to_all | solution.py:35
  626.6 4.5 all-to-all-start.5
  637.2 4.2 broadcast_in_dim_reshape.9
  646.7 50.3 %all-to-all-done.5 = f32[352,8,256]{2,0,1:T(8,128)} async-done(((f32[352,8,256]{2,0,1:T(8,128)}), f32[352,8,256]{2,0,1:T(8,128)}, u32[]{:S(2)}, u32[]{:S(2)}) %all-to-all-start.5) | async-done | bytes 2883616 | tf_op jit(solution)/shard_map/all_to_all | solution.py:35
  696.9 3.5 copy.41
  702.2 6.3 copy.48
  (44 shorter events, 39.7 us)
Async XLA Ops:
  8.0 1.9 copy-start
  8.0 143.1 %reduce-scatter.4.cloned.1.call-start = ((), (), s32[]{:S(2)}) async-start(), calls=%async_computation.9 | async-start | bytes 14417920
  34.8 0.7 copy-start.6
  34.8 3.0 copy-start.4
  34.8 178.7 %all-reduce.2.cloned.1.call-start = ((), (), s32[]{:S(2)}) async-start(), calls=%async_computation.7 | async-start | bytes 1048576 | tf_op jit(solution)/shard_map/psum | solution.py:81
  40.1 3.6 copy-start.5
  266.6 4.7 copy-start.3
  266.6 70.6 %all-to-all-start = ((f32[352,8,256]{2,0,1:T(8,128)}), f32[352,8,256]{2,0,1:T(8,128)}, u32[]{:S(2)}, u32[]{:S(2)}) async-start(f32[352,8,256]{2,0,1:T(8,128)} %copy.35), calls=%async_computation | async-start | bytes 5767168 | tf_op jit(solution)/shard_map/all_to_all | solution.py:39
  273.5 68.1 %copy-start.2 = (f32[352,2048]{0,1:T(8,128)S(1)}, f32[352,2048]{0,1:T(8,128)}, u32[]{:S(2)}) copy-start(f32[352,2048]{0,1:T(8,128)} %get-tuple-element.13) | copy-start | bytes 8650756
  337.1 70.3 %all-to-all-start.2 = ((f32[352,8,256]{2,0,1:T(8,128)}), f32[352,8,256]{2,0,1:T(8,128)}, u32[]{:S(2)}, u32[]{:S(2)}) async-start(f32[352,8,256]{2,0,1:T(8,128)} %copy.38), calls=%async_computation.2 | async-start | bytes 5767168 | tf_op jit(solution)/shard_map/all_to_all | solution.py:40
  343.9 68.2 %copy-start.7 = (s32[8]{0:T(128)S(1)}, s32[8]{0:T(128)}, u32[]{:S(2)}) copy-start(s32[8]{0:T(128)} %param.25) | copy-start | bytes 100
  407.5 70.3 %all-to-all-start.4 = ((f32[352,8,256]{2,0,1:T(8,128)}), f32[352,8,256]{2,0,1:T(8,128)}, u32[]{:S(2)}, u32[]{:S(2)}) async-start(f32[352,8,256]{2,0,1:T(8,128)} %copy.40), calls=%async_computation.4 | async-start | bytes 5767168 | tf_op jit(solution)/shard_map/all_to_all | solution.py:41
  556.3 70.3 %all-to-all-start.3 = ((f32[352,8,256]{2,0,1:T(8,128)}), f32[352,8,256]{2,0,1:T(8,128)}, u32[]{:S(2)}, u32[]{:S(2)}) async-start(f32[352,8,256]{2,0,1:T(8,128)} %get-tuple-element.15), calls=%async_computation.3 | async-start | bytes 5767168 | tf_op jit(solution)/shard_map/all_to_all | solution.py:35
  560.7 141.6 %all-gather.2.cloned.1.call-start = ((), (), s32[]{:S(2)}) async-start(), calls=%async_computation.8 | async-start | bytes 7208960 | tf_op jit(solution)/shard_map/all_gather | solution.py:48
  626.6 70.4 %all-to-all-start.5 = ((f32[352,8,256]{2,0,1:T(8,128)}), f32[352,8,256]{2,0,1:T(8,128)}, u32[]{:S(2)}, u32[]{:S(2)}) async-start(f32[352,8,256]{2,0,1:T(8,128)} %get-tuple-element.14), calls=%async_computation.5 | async-start | bytes 5767168 | tf_op jit(solution)/shard_map/all_to_all | solution.py:35
  702.2 6.3 copy-start.1
Sparse Core Ops, SparseCore 0:
  35.0 116.1 reduce-scatter.3
  563.9 67.7 all-gather.1
Sparse Core Ops, SparseCore 1:
  41.2 172.3 all-reduce.1
where the time goes:
time: 717 us; the launch traced here: 716 us
  waiting for transfers between devices  465 us (65%)
  blocking collectives  108 us (15%)
  local copies, waits for them, and re-layouts  68.8 us (10%)
  starting transfers between devices  22.7 us (3%)
  other arithmetic  19.2 us (3%)
  between operations  17.8 us (2%)
  matrix products  15.1 us (2%)
    all_to_all x2, waiting for transfers between devices, reorder(): lax.all_to_all(arranged, 'expert', split_axis=1, concat_axis=1, tiled=True)  115 us
    unnamed x4, waiting for transfers between devices  105 us
    all_to_all x1, blocking collectives, reorder(): lax.all_to_all(arranged, 'expert', split_axis=1, concat_axis=1, tiled=True)  68.3 us
    all_to_all x1, waiting for transfers between devices, relocate_state(): lax.all_to_all(pieces[1], 'expert', split_axis=1, concat_axis=1, tiled=True)  63.6 us
    all_to_all x1, waiting for transfers between devices, relocate_state(): lax.all_to_all(pieces[0], 'expert', split_axis=1, concat_axis=1, tiled=True)  63.6 us
    all_to_all x1, waiting for transfers between devices, relocate_state(): lax.all_to_all(pieces[2], 'expert', split_axis=1, concat_axis=1, tiled=True)  59 us
    psum x1, waiting for transfers between devices, on_device(): lax.psum((router_partial, jnp.sum(gradient * gradient)), ('dp', 'expert'))  58.7 us
    psum x1, blocking collectives, on_device(): lax.psum((router_partial, jnp.sum(gradient * gradient)), ('dp', 'expert'))  39.5 us
  transfers between devices with their start and end apart: 8, of which 7 were waited for; matrix products, arithmetic and copies ran while one was open for 7% of the time, Pallas kernels for 0%

commit v1 on v0

--- a/solution.py
+++ b/solution.py
@@ -79,7 +79,7 @@
         tiled=True,
     )
     router_grad, expert_square = lax.psum(
-        (router_partial, jnp.sum(gradient * gradient)), ("dp", "expert")
+        lax.psum((router_partial, jnp.sum(gradient * gradient)), "expert"), "dp"
     )
     total_square = expert_square + jnp.sum(router_grad * router_grad)
     clip_limit = 2.0 * math.sqrt(

time: 717 us -> 673 us (0.939)
  waiting for transfers between devices: 465 us -> 433 us
  blocking collectives: 108 us -> 94.6 us
    unnamed x4 -> x5, waiting for transfers between devices: 105 us -> 73.8 us
    psum x1 -> x2, blocking collectives: 39.5 us -> 26.3 us  [the longest x1 16.8 us: on_device(): lax.psum((router_partial, jnp.sum(gradient * gradient)), 'expert')]
    unnamed x22 -> x18, local copies, waits for them, and re-layouts: 30.8 us -> 30 us
    psum x1 -> x2, waiting for transfers between devices: 58.7 us -> 58.7 us  [the longest x1 35 us: on_device(): lax.psum((router_partial, jnp.sum(gradient * gradient)), 'expert')]
  transfers between devices with their start and end apart: 8 -> 9, of which waited for: 7 -> 8; matrix products, arithmetic and copies ran while one was open for 7% -> 11% of each run, Pallas kernels for 0% -> 0%
where the time goes in v1:
time: 673 us; the launch traced here: 671 us
  waiting for transfers between devices  433 us (64%)
  blocking collectives  94.6 us (14%)
  local copies, waits for them, and re-layouts  68.1 us (10%)
  starting transfers between devices  23 us (3%)
  other arithmetic  19.2 us (3%)
  between operations  17.8 us (3%)
  matrix products  15.1 us (2%)
    all_to_all x2, waiting for transfers between devices, reorder(): lax.all_to_all(arranged, 'expert', split_axis=1, concat_axis=1, tiled=True)  115 us
    unnamed x5, waiting for transfers between devices  73.8 us
    all_to_all x1, blocking collectives, reorder(): lax.all_to_all(arranged, 'expert', split_axis=1, concat_axis=1, tiled=True)  68.3 us
    all_to_all x1, waiting for transfers between devices, relocate_state(): lax.all_to_all(pieces[0], 'expert', split_axis=1, concat_axis=1, tiled=True)  63.7 us
    all_to_all x1, waiting for transfers between devices, relocate_state(): lax.all_to_all(pieces[1], 'expert', split_axis=1, concat_axis=1, tiled=True)  63.6 us
    all_to_all x1, waiting for transfers between devices, relocate_state(): lax.all_to_all(pieces[2], 'expert', split_axis=1, concat_axis=1, tiled=True)  59 us
    psum x1, waiting for transfers between devices, on_device(): lax.psum((router_partial, jnp.sum(gradient * gradient)), 'expert')  35 us
    unnamed x18, local copies, waits for them, and re-layouts  30 us
  transfers between devices with their start and end apart: 9, of which 8 were waited for; matrix products, arithmetic and copies ran while one was open for 11% of the time, Pallas kernels for 0%

profile of v1, /device:TPU:0, one launch (start us, length us, event | category | flops | bytes accessed | tf_op | source)
XLA Modules:
  0.0 671.3 jit_solution(11135036594333607445)
XLA Ops:
  11.0 12.9 %convolution_bitcast_fusion = f32[1408,2048]{0,1:T(8,128)} fusion(bf16[1,1152,2048]{2,1,0:T(8,128)(2,1)} %param.15, pred[1152]{0:T(1024)(128)(4,1)S(1)} %iota_compare_fusion, bf16[1,1152,1408]{2,1,0:T(8,128)(2,1)S(1)} %copy-done), kind=kOutput, calls=%fused_computation.3 | convolution fusion | flops 6646136832 | bytes 19498112 | tf_op jit(solution)/shard_map/dot_general | solution.py:74
  23.9 12.0 %copy.42 = f32[1408,2048]{1,0:T(8,128)} copy(f32[1408,2048]{0,1:T(8,128)} %convolution_bitcast_fusion) | data formatting | bytes 23068672
  36.0 35.0 %all-reduce.3.cloned.1.call-done = f32[64,2048]{1,0:T(8,128)} async-done(((f32[64,2048]{1,0:T(8,128)}), f32[64,2048]{1,0:T(8,128)}) %all-reduce.3.cloned.1.call-update) | async-done | bytes 524304 | tf_op jit(solution)/shard_map/psum | solution.py:82
  76.9 73.8 %reduce-scatter.4.cloned.1.call-done = f32[352,2048]{1,0:T(8,128)} async-done(((f32[1408,2048]{1,0:T(8,128)}), f32[352,2048]{1,0:T(8,128)}) %reduce-scatter.4.cloned.1.call-update) | async-done | bytes 2883600
  157.9 16.8 %psum.28 = f32[]{:T(128)} all-reduce(f32[]{:T(128)} %multiply_reduce_fusion), channel_id=1, replica_groups=mesh['dp'=4,'expert'=8] {'expert'}, use_global_device_ids=true, to_apply=%region_2.3 | all-reduce | flops 1 | bytes 8 | tf_op jit(solution)/shard_map/psum | solution.py:82
  174.7 23.7 %all-reduce.5.cloned.1.call-done = f32[64,2048]{1,0:T(8,128)} async-done(((f32[64,2048]{1,0:T(8,128)}), f32[64,2048]{1,0:T(8,128)}) %all-reduce.5.cloned.1.call-update) | async-done | bytes 524304 | tf_op jit(solution)/shard_map/psum | solution.py:81
  200.2 9.5 %psum.29 = f32[]{:T(128)} all-reduce(f32[]{:T(128)} %psum.28), channel_id=1, replica_groups=mesh['dp'=4,'expert'=8] {'dp'}, use_global_device_ids=true, to_apply=%region_3.4 | all-reduce | flops 1 | bytes 8 | tf_op jit(solution)/shard_map/psum | solution.py:81
  211.1 6.9 %bitcast_subtract_fusion = (f32[352,2048]{0,1:T(8,128)}, f32[352,2048]{0,1:T(8,128)}, f32[352,2048]{0,1:T(8,128)}) fusion(f32[1,352,2048]{1,2,0:T(8,128)} %copy.32, f32[352,2048]{0,1:T(8,128)S(1)} %copy.43, f32[]{:T(128)S(6)} %min_shard_map.3, f32[1,352,2048]{1,2,0:T(8,128)} %copy.33, f32[1,352,2048]{1,2,0:T(8,128)} %copy.34), kind=kLoop, calls=%fused_computation.11 | loop fusion | flops 11534336 | bytes 20185092 | tf_op jit(solution)/shard_map/sub | solution.py:21
  221.4 4.9 all-to-all-start
  228.6 63.7 %all-to-all-done = f32[352,8,256]{2,0,1:T(8,128)} async-done(((f32[352,8,256]{2,0,1:T(8,128)}), f32[352,8,256]{2,0,1:T(8,128)}, u32[]{:S(2)}, u32[]{:S(2)}) %all-to-all-start) | async-done | bytes 2883616 | tf_op jit(solution)/shard_map/all_to_all | solution.py:39
  292.3 4.4 all-to-all-start.2
  299.0 63.6 %all-to-all-done.2 = f32[352,8,256]{2,0,1:T(8,128)} async-done(((f32[352,8,256]{2,0,1:T(8,128)}), f32[352,8,256]{2,0,1:T(8,128)}, u32[]{:S(2)}, u32[]{:S(2)}) %all-to-all-start.2) | async-done | bytes 2883616 | tf_op jit(solution)/shard_map/all_to_all | solution.py:40
  362.6 4.6 all-to-all-start.4
  369.8 4.1 gather_fusion.1
  373.9 59.0 %all-to-all-done.4 = f32[352,8,256]{2,0,1:T(8,128)} async-done(((f32[352,8,256]{2,0,1:T(8,128)}), f32[352,8,256]{2,0,1:T(8,128)}, u32[]{:S(2)}, u32[]{:S(2)}) %all-to-all-start.4) | async-done | bytes 2883616 | tf_op jit(solution)/shard_map/all_to_all | solution.py:41
  432.9 4.1 gather_fusion.2
  437.0 6.0 select_bitcast_fusion
  443.1 68.3 %all_to_all.30 = f32[352,8,256]{2,0,1:T(8,128)S(1)} all-to-all(f32[352,8,256]{2,0,1:T(8,128)S(1)} %get-tuple-element.16), channel_id=1, replica_groups=mesh['dp'=4,'expert'=8] {'expert'}, dimensions={1} | all-to-all | bytes 5767168 | tf_op jit(solution)/shard_map/all_to_all | solution.py:35
  511.4 4.4 all-to-all-start.3
  517.4 64.4 %all-to-all-done.3 = f32[352,8,256]{2,0,1:T(8,128)} async-done(((f32[352,8,256]{2,0,1:T(8,128)}), f32[352,8,256]{2,0,1:T(8,128)}, u32[]{:S(2)}, u32[]{:S(2)}) %all-to-all-start.3) | async-done | bytes 2883616 | tf_op jit(solution)/shard_map/all_to_all | solution.py:35
  581.7 4.5 all-to-all-start.5
  592.4 4.2 broadcast_in_dim_reshape.9
  601.8 50.3 %all-to-all-done.5 = f32[352,8,256]{2,0,1:T(8,128)} async-done(((f32[352,8,256]{2,0,1:T(8,128)}), f32[352,8,256]{2,0,1:T(8,128)}, u32[]{:S(2)}, u32[]{:S(2)}) %all-to-all-start.5) | async-done | bytes 2883616 | tf_op jit(solution)/shard_map/all_to_all | solution.py:35
  657.4 6.3 copy.49
  (44 shorter events, 46.1 us)
Async XLA Ops:
  8.0 3.0 copy-start
  8.0 63.0 %all-reduce.3.cloned.1.call-start = ((), (), s32[]{:S(2)}) async-start(), calls=%async_computation.7 | async-start | bytes 1048576 | tf_op jit(solution)/shard_map/psum | solution.py:82
  10.3 140.4 %reduce-scatter.4.cloned.1.call-start = ((), (), s32[]{:S(2)}) async-start(), calls=%async_computation.10 | async-start | bytes 14417920
  35.9 35.1 %copy-start.4 = (f32[1,352,2048]{2,1,0:T(8,128)S(1)}, f32[1,352,2048]{2,1,0:T(8,128)}, u32[]{:S(2)}) copy-start(f32[1,352,2048]{2,1,0:T(8,128)} %param.17) | copy-start | bytes 8650756
  35.9 162.4 %all-reduce.5.cloned.1.call-start = ((), (), s32[]{:S(2)}) async-start(), calls=%async_computation.8 | async-start | bytes 1048576 | tf_op jit(solution)/shard_map/psum | solution.py:81
  221.4 4.9 copy-start.3
  221.4 70.9 %all-to-all-start = ((f32[352,8,256]{2,0,1:T(8,128)}), f32[352,8,256]{2,0,1:T(8,128)}, u32[]{:S(2)}, u32[]{:S(2)}) async-start(f32[352,8,256]{2,0,1:T(8,128)} %copy.35), calls=%async_computation | async-start | bytes 5767168 | tf_op jit(solution)/shard_map/all_to_all | solution.py:39
  228.6 68.2 %copy-start.2 = (f32[352,2048]{0,1:T(8,128)S(1)}, f32[352,2048]{0,1:T(8,128)}, u32[]{:S(2)}) copy-start(f32[352,2048]{0,1:T(8,128)} %get-tuple-element.13) | copy-start | bytes 8650756
  292.3 70.3 %all-to-all-start.2 = ((f32[352,8,256]{2,0,1:T(8,128)}), f32[352,8,256]{2,0,1:T(8,128)}, u32[]{:S(2)}, u32[]{:S(2)}) async-start(f32[352,8,256]{2,0,1:T(8,128)} %copy.38), calls=%async_computation.2 | async-start | bytes 5767168 | tf_op jit(solution)/shard_map/all_to_all | solution.py:40
  299.0 68.2 %copy-start.5 = (s32[8]{0:T(128)S(1)}, s32[8]{0:T(128)}, u32[]{:S(2)}) copy-start(s32[8]{0:T(128)} %param.25) | copy-start | bytes 100
  362.6 70.3 %all-to-all-start.4 = ((f32[352,8,256]{2,0,1:T(8,128)}), f32[352,8,256]{2,0,1:T(8,128)}, u32[]{:S(2)}, u32[]{:S(2)}) async-start(f32[352,8,256]{2,0,1:T(8,128)} %copy.40), calls=%async_computation.4 | async-start | bytes 5767168 | tf_op jit(solution)/shard_map/all_to_all | solution.py:41
  511.4 70.3 %all-to-all-start.3 = ((f32[352,8,256]{2,0,1:T(8,128)}), f32[352,8,256]{2,0,1:T(8,128)}, u32[]{:S(2)}, u32[]{:S(2)}) async-start(f32[352,8,256]{2,0,1:T(8,128)} %get-tuple-element.15), calls=%async_computation.3 | async-start | bytes 5767168 | tf_op jit(solution)/shard_map/all_to_all | solution.py:35
  515.9 141.5 %all-gather.2.cloned.1.call-start = ((), (), s32[]{:S(2)}) async-start(), calls=%async_computation.9 | async-start | bytes 7208960 | tf_op jit(solution)/shard_map/all_gather | solution.py:48
  581.7 70.4 %all-to-all-start.5 = ((f32[352,8,256]{2,0,1:T(8,128)}), f32[352,8,256]{2,0,1:T(8,128)}, u32[]{:S(2)}, u32[]{:S(2)}) async-start(f32[352,8,256]{2,0,1:T(8,128)} %get-tuple-element.14), calls=%async_computation.5 | async-start | bytes 5767168 | tf_op jit(solution)/shard_map/all_to_all | solution.py:35
  657.4 6.3 copy-start.1
Sparse Core Ops, SparseCore 0:
  11.7 59.2 all-reduce.2
Sparse Core Ops, SparseCore 1:
  36.0 114.6 reduce-scatter.3
  153.6 44.8 all-reduce.4
  518.8 65.9 all-gather.1
